TPU v7x, 8 devices: a whole 2x2x1 slice. The times are simulated.
8 devices in a mesh: batch: 1 (over z), row: 8 (over y, x, core).
Axes of the slice: x: 2, y: 2, z: 1, core: 2. Of those that a mesh axis runs over, the one named last changes fastest.
Arguments:
- trans_mat: bfloat16 [16384, 16384], P(('batch', 'row'))
- teleport: float32 [16384, 256], P(('batch', 'row'))
- dangling: int32 [16384], P(('batch', 'row'))
- damping: float32 [8], replicated
- rank_init: float32 [16384, 256], P(('batch', 'row'))
Outputs:
- output: float32 [16384, 256], P(('batch', 'row'))
All inputs are finite; a program needn't handle non-finite values.
Results may differ from a plain program's by a relative error of at most 0.001.
Values are sent between devices in bfloat16 or wider.
A program may use at most 1 GiB of HBM per device.

v0:
```python
import jax
import jax.numpy as jnp
from jax import lax
from jax.sharding import PartitionSpec as P, NamedSharding


def solution(mesh):
    spec_rows = P(("batch", "row"), None)
    spec_vec = P(("batch", "row"))

    def local_sweeps(mat_rows, tele_rows, dang_rows, damping, start_rows):
        num_nodes = mat_rows.shape[1]
        dang_float = dang_rows.astype(jnp.float32)
        rank_rows = start_rows
        for sweep_idx in range(damping.shape[0]):
            gathered = lax.all_gather(rank_rows.astype(jnp.bfloat16), "row", axis=0, tiled=True)
            dang_mass = lax.psum(jnp.dot(dang_float, rank_rows, preferred_element_type=jnp.float32), "row")
            prod_rows = jnp.dot(mat_rows, gathered, preferred_element_type=jnp.float32)
            factor = damping[sweep_idx]
            rank_rows = factor * prod_rows + (1.0 - factor) * tele_rows + (factor / num_nodes) * dang_mass[None, :]
        return rank_rows

    sharded_fn = jax.shard_map(local_sweeps, mesh=mesh, in_specs=(spec_rows, spec_rows, spec_vec, P(None), spec_rows), out_specs=spec_rows, check_vma=False)
    return sharded_fn
```

profile of v0, /device:TPU:0, one launch (start us, length us, event | category | flops | bytes accessed | tf_op | source)
XLA Modules:
  0.0 654.8 jit_solution(14241975345675584655)
XLA Ops:
  6.5 0.0 copy-start
  6.5 0.0 copy-start.5
  6.5 0.0 copy-start.4
  6.5 0.0 all-gather.9.cloned.1.call-start
  6.5 2.8 convert_element_type.27
  9.4 0.0 all-gather.9.cloned.1.call-update
  9.4 0.0 all-gather.11.cloned.1.call-start
  9.4 0.0 copy-done.5
  9.4 0.0 copy-done.4
  9.5 0.7 fusion.23
  11.4 0.0 copy-done
  11.4 0.2 fusion.24
  11.7 25.5 %psum.56 = f32[256]{0:T(256)S(1)} all-reduce(f32[256]{0:T(256)S(1)} %bitcast.107), channel_id=1, replica_groups=mesh['batch'=1,'row'=8] {'row'}, use_global_device_ids=true, to_apply=%region_0.0 | all-reduce | flops 256 | bytes 2048 | tf_op jit(solution)/shard_map/psum | solution.py:17
  37.2 24.0 %all-gather.9.cloned.1.call-done = bf16[16384,256]{1,0:T(8,128)(2,1)} async-done(((bf16[2048,256]{1,0:T(8,128)(2,1)}), bf16[16384,256]{1,0:T(8,128)(2,1)}) %all-gather.9.cloned.1.call-update) | async-done | bytes 8388624 | tf_op jit(solution)/shard_map/all_gather | solution.py:16
  61.2 0.0 copy-start.2
  61.2 32.1 %fusion.8 = bf16[2048,256]{1,0:T(8,128)(2,1)} fusion(bf16[2048,16384]{1,0:T(8,128)(2,1)} %param.5, bf16[16384,256]{1,0:T(8,128)(2,1)} %all-gather.9.cloned.1.call-done, f32[2048,256]{1,0:T(8,128)} %param.6, f32[256]{0:T(256)S(1)} %broadcast_multiply_fusion.7, f32[]{:T(128)S(6)} %sub.24, f32[]{:T(128)} %bitcast.7), kind=kOutput, calls=%fused_computation.16 | convolution fusion | flops 17182490624 | bytes 78644232 | tf_op jit(solution)/shard_map/dot_general | solution.py:18
  93.3 0.0 all-gather.11.cloned.1.call-update
  93.4 0.0 all-gather.13.cloned.1.call-start
  94.7 0.0 copy-done.2
  94.7 0.0 copy-start.1
  94.7 1.8 copy.6
  96.5 0.0 copy-done.1
  96.5 0.2 fusion.25
  96.7 22.7 %psum.57 = f32[256]{0:T(256)S(1)} all-reduce(f32[256]{0:T(256)S(1)} %bitcast.108), channel_id=1, replica_groups=mesh['batch'=1,'row'=8] {'row'}, use_global_device_ids=true, to_apply=%region_1.0 | all-reduce | flops 256 | bytes 2048 | tf_op jit(solution)/shard_map/psum | solution.py:17
  119.5 23.3 %all-gather.11.cloned.1.call-done = bf16[16384,256]{1,0:T(8,128)(2,1)} async-done(((bf16[2048,256]{1,0:T(8,128)(2,1)}), bf16[16384,256]{1,0:T(8,128)(2,1)}) %all-gather.11.cloned.1.call-update) | async-done | bytes 8388624 | tf_op jit(solution)/shard_map/all_gather | solution.py:16
  142.8 29.9 %fusion.10 = bf16[2048,256]{0,1:T(8,128)(2,1)} fusion(bf16[16384,256]{1,0:T(8,128)(2,1)} %all-gather.11.cloned.1.call-done, bf16[2048,16384]{1,0:T(8,128)(2,1)} %param.5, f32[2048,256]{0,1:T(8,128)} %copy.6, f32[256]{0:T(256)S(1)} %broadcast_multiply_fusion.6, f32[]{:T(128)S(6)} %sub.25, f32[]{:T(128)} %bitcast.6), kind=kOutput, calls=%fused_computation.18 | convolution fusion | flops 17182490624 | bytes 78644232 | tf_op jit(solution)/shard_map/dot_general | solution.py:18
  172.7 0.0 copy-start.3
  172.7 0.0 all-gather.13.cloned.1.call-update
  172.7 0.0 all-gather.15.cloned.1.call-start
  174.3 1.6 fusion.26
  175.9 22.7 %psum.58 = f32[256]{0:T(256)S(1)} all-reduce(f32[256]{0:T(256)S(1)} %bitcast.109), channel_id=1, replica_groups=mesh['batch'=1,'row'=8] {'row'}, use_global_device_ids=true, to_apply=%region_2.0 | all-reduce | flops 256 | bytes 2048 | tf_op jit(solution)/shard_map/psum | solution.py:17
  198.6 23.3 %all-gather.13.cloned.1.call-done = bf16[16384,256]{0,1:T(8,128)(2,1)} async-done(((bf16[2048,256]{0,1:T(8,128)(2,1)}), bf16[16384,256]{0,1:T(8,128)(2,1)}) %all-gather.13.cloned.1.call-update) | async-done | bytes 8388624 | tf_op jit(solution)/shard_map/all_gather | solution.py:16
  222.0 0.0 copy-done.3
  222.0 29.4 %fusion.12 = bf16[2048,256]{0,1:T(8,128)(2,1)} fusion(bf16[16384,256]{0,1:T(8,128)(2,1)} %all-gather.13.cloned.1.call-done, bf16[2048,16384]{1,0:T(8,128)(2,1)} %param.5, f32[2048,256]{0,1:T(8,128)S(1)} %copy-done.3, f32[256]{0:T(256)S(1)} %broadcast_multiply_fusion.5, f32[]{:T(128)S(6)} %sub.26, f32[]{:T(128)} %bitcast.5), kind=kOutput, calls=%fused_computation.20 | convolution fusion | flops 17182490624 | bytes 78644232 | tf_op jit(solution)/shard_map/dot_general | solution.py:18
  251.3 0.0 all-gather.15.cloned.1.call-update
  251.4 0.0 all-gather.17.cloned.1.call-start
  252.5 1.6 fusion.27
  254.1 22.7 %psum.59 = f32[256]{0:T(256)S(1)} all-reduce(f32[256]{0:T(256)S(1)} %bitcast.110), channel_id=1, replica_groups=mesh['batch'=1,'row'=8] {'row'}, use_global_device_ids=true, to_apply=%region_3.0 | all-reduce | flops 256 | bytes 2048 | tf_op jit(solution)/shard_map/psum | solution.py:17
  276.8 23.8 %all-gather.15.cloned.1.call-done = bf16[16384,256]{0,1:T(8,128)(2,1)} async-done(((bf16[2048,256]{0,1:T(8,128)(2,1)}), bf16[16384,256]{0,1:T(8,128)(2,1)}) %all-gather.15.cloned.1.call-update) | async-done | bytes 8388624 | tf_op jit(solution)/shard_map/all_gather | solution.py:16
  300.6 29.3 %fusion.14 = bf16[2048,256]{0,1:T(8,128)(2,1)} fusion(bf16[16384,256]{0,1:T(8,128)(2,1)} %all-gather.15.cloned.1.call-done, bf16[2048,16384]{1,0:T(8,128)(2,1)} %param.5, f32[2048,256]{0,1:T(8,128)S(1)} %copy-done.3, f32[256]{0:T(256)S(1)} %broadcast_multiply_fusion.4, f32[]{:T(128)S(6)} %sub.27, f32[]{:T(128)} %bitcast.4), kind=kOutput, calls=%fused_computation.22 | convolution fusion | flops 17182490624 | bytes 78644232 | tf_op jit(solution)/shard_map/dot_general | solution.py:18
  329.9 0.0 all-gather.17.cloned.1.call-update
  329.9 0.0 all-gather.19.cloned.1.call-start
  331.2 1.6 fusion.28
  332.8 22.7 %psum.60 = f32[256]{0:T(256)S(1)} all-reduce(f32[256]{0:T(256)S(1)} %bitcast.111), channel_id=1, replica_groups=mesh['batch'=1,'row'=8] {'row'}, use_global_device_ids=true, to_apply=%region_4.0 | all-reduce | flops 256 | bytes 2048 | tf_op jit(solution)/shard_map/psum | solution.py:17
  355.5 23.7 %all-gather.17.cloned.1.call-done = bf16[16384,256]{0,1:T(8,128)(2,1)} async-done(((bf16[2048,256]{0,1:T(8,128)(2,1)}), bf16[16384,256]{0,1:T(8,128)(2,1)}) %all-gather.17.cloned.1.call-update) | async-done | bytes 8388624 | tf_op jit(solution)/shard_map/all_gather | solution.py:16
  379.3 29.3 %fusion.16 = bf16[2048,256]{0,1:T(8,128)(2,1)} fusion(bf16[16384,256]{0,1:T(8,128)(2,1)} %all-gather.17.cloned.1.call-done, bf16[2048,16384]{1,0:T(8,128)(2,1)} %param.5, f32[2048,256]{0,1:T(8,128)S(1)} %copy-done.3, f32[256]{0:T(256)S(1)} %broadcast_multiply_fusion.3, f32[]{:T(128)S(6)} %sub.28, f32[]{:T(128)} %bitcast.3), kind=kOutput, calls=%fused_computation.24 | convolution fusion | flops 17182490624 | bytes 78644232 | tf_op jit(solution)/shard_map/dot_general | solution.py:18
  408.6 0.0 all-gather.19.cloned.1.call-update
  408.6 0.3 all-gather.21.cloned.1.call-start
  410.1 1.6 fusion.29
  411.7 22.7 %psum.61 = f32[256]{0:T(256)S(1)} all-reduce(f32[256]{0:T(256)S(1)} %bitcast.112), channel_id=1, replica_groups=mesh['batch'=1,'row'=8] {'row'}, use_global_device_ids=true, to_apply=%region_5.0 | all-reduce | flops 256 | bytes 2048 | tf_op jit(solution)/shard_map/psum | solution.py:17
  434.5 23.5 %all-gather.19.cloned.1.call-done = bf16[16384,256]{0,1:T(8,128)(2,1)} async-done(((bf16[2048,256]{0,1:T(8,128)(2,1)}), bf16[16384,256]{0,1:T(8,128)(2,1)}) %all-gather.19.cloned.1.call-update) | async-done | bytes 8388624 | tf_op jit(solution)/shard_map/all_gather | solution.py:16
  457.9 29.3 %fusion.18 = bf16[2048,256]{0,1:T(8,128)(2,1)} fusion(bf16[16384,256]{0,1:T(8,128)(2,1)} %all-gather.19.cloned.1.call-done, bf16[2048,16384]{1,0:T(8,128)(2,1)} %param.5, f32[2048,256]{0,1:T(8,128)S(1)} %copy-done.3, f32[256]{0:T(256)S(1)} %broadcast_multiply_fusion.2, f32[]{:T(128)S(6)} %sub.29, f32[]{:T(128)} %bitcast.2), kind=kOutput, calls=%fused_computation.26 | convolution fusion | flops 17182490624 | bytes 78644232 | tf_op jit(solution)/shard_map/dot_general | solution.py:18
  487.2 0.0 all-gather.21.cloned.1.call-update
  487.3 0.0 all-gather.23.cloned.1.call-start
  488.7 1.6 fusion.30
  490.3 22.7 %psum.62 = f32[256]{0:T(256)S(1)} all-reduce(f32[256]{0:T(256)S(1)} %bitcast.113), channel_id=1, replica_groups=mesh['batch'=1,'row'=8] {'row'}, use_global_device_ids=true, to_apply=%region_6.0 | all-reduce | flops 256 | bytes 2048 | tf_op jit(solution)/shard_map/psum | solution.py:17
  513.0 23.6 %all-gather.21.cloned.1.call-done = bf16[16384,256]{0,1:T(8,128)(2,1)} async-done(((bf16[2048,256]{0,1:T(8,128)(2,1)}), bf16[16384,256]{0,1:T(8,128)(2,1)}) %all-gather.21.cloned.1.call-update) | async-done | bytes 8388624 | tf_op jit(solution)/shard_map/all_gather | solution.py:16
  536.6 29.4 %fusion.20 = bf16[2048,256]{0,1:T(8,128)(2,1)} fusion(bf16[16384,256]{0,1:T(8,128)(2,1)} %all-gather.21.cloned.1.call-done, bf16[2048,16384]{1,0:T(8,128)(2,1)} %param.5, f32[2048,256]{0,1:T(8,128)S(1)} %copy-done.3, f32[256]{0:T(256)S(1)} %broadcast_multiply_fusion.1, f32[]{:T(128)S(6)} %sub.30, f32[]{:T(128)} %bitcast.1), kind=kOutput, calls=%fused_computation.28 | convolution fusion | flops 17182490624 | bytes 78644232 | tf_op jit(solution)/shard_map/dot_general | solution.py:18
  566.0 0.0 all-gather.23.cloned.1.call-update
  567.4 1.6 fusion.31
  569.0 23.0 %psum.63 = f32[256]{0:T(256)S(1)} all-reduce(f32[256]{0:T(256)S(1)} %bitcast.106), channel_id=1, replica_groups=mesh['batch'=1,'row'=8] {'row'}, use_global_device_ids=true, to_apply=%region_7.0 | all-reduce | flops 256 | bytes 2048 | tf_op jit(solution)/shard_map/psum | solution.py:17
  592.0 23.4 %all-gather.23.cloned.1.call-done = bf16[16384,256]{0,1:T(8,128)(2,1)} async-done(((bf16[2048,256]{0,1:T(8,128)(2,1)}), bf16[16384,256]{0,1:T(8,128)(2,1)}) %all-gather.23.cloned.1.call-update) | async-done | bytes 8388624 | tf_op jit(solution)/shard_map/all_gather | solution.py:16
  615.4 29.7 %fusion.22 = f32[2048,256]{0,1:T(8,128)} fusion(bf16[16384,256]{0,1:T(8,128)(2,1)} %all-gather.23.cloned.1.call-done, bf16[2048,16384]{1,0:T(8,128)(2,1)} %param.5, f32[2048,256]{0,1:T(8,128)S(1)} %copy-done.3, f32[256]{0:T(256)S(1)} %broadcast_multiply_fusion, f32[]{:T(128)S(6)} %sub.31, f32[]{:T(128)} %bitcast), kind=kOutput, calls=%fused_computation.30 | convolution fusion | flops 17181966336 | bytes 79692808 | tf_op jit(solution)/shard_map/dot_general | solution.py:18
  645.1 2.9 copy.13
  (9 shorter events, 0.0 us)
Async XLA Ops:
  6.5 4.9 copy-start
  6.5 2.9 copy-start.5
  6.5 2.9 copy-start.4
  6.5 54.7 %all-gather.9.cloned.1.call-start = ((), (), s32[]{:S(2)}) async-start(), calls=%async_computation | async-start | bytes 9437184 | tf_op jit(solution)/shard_map/all_gather | solution.py:16
  9.4 133.4 %all-gather.11.cloned.1.call-start = ((), (), s32[]{:S(2)}) async-start(), calls=%async_computation.1 | async-start | bytes 9437184 | tf_op jit(solution)/shard_map/all_gather | solution.py:16
  61.2 33.4 %copy-start.2 = (f32[2048,256]{1,0:T(8,128)S(1)}, f32[2048,256]{1,0:T(8,128)}, u32[]{:S(2)}) copy-start(f32[2048,256]{1,0:T(8,128)} %param.6) | copy-start | bytes 6291460
  93.4 128.6 %all-gather.13.cloned.1.call-start = ((), (), s32[]{:S(2)}) async-start(), calls=%async_computation.2 | async-start | bytes 9437184 | tf_op jit(solution)/shard_map/all_gather | solution.py:16
  94.7 1.8 copy-start.1
  172.7 49.3 %copy-start.3 = (f32[2048,256]{0,1:T(8,128)S(1)}, f32[2048,256]{0,1:T(8,128)}, u32[]{:S(2)}) copy-start(f32[2048,256]{0,1:T(8,128)} %copy.6) | copy-start | bytes 6291460
  172.7 127.9 %all-gather.15.cloned.1.call-start = ((), (), s32[]{:S(2)}) async-start(), calls=%async_computation.3 | async-start | bytes 9437184 | tf_op jit(solution)/shard_map/all_gather | solution.py:16
  251.4 127.9 %all-gather.17.cloned.1.call-start = ((), (), s32[]{:S(2)}) async-start(), calls=%async_computation.4 | async-start | bytes 9437184 | tf_op jit(solution)/shard_map/all_gather | solution.py:16
  329.9 128.0 %all-gather.19.cloned.1.call-start = ((), (), s32[]{:S(2)}) async-start(), calls=%async_computation.5 | async-start | bytes 9437184 | tf_op jit(solution)/shard_map/all_gather | solution.py:16
  408.6 128.0 %all-gather.21.cloned.1.call-start = ((), (), s32[]{:S(2)}) async-start(), calls=%async_computation.6 | async-start | bytes 9437184 | tf_op jit(solution)/shard_map/all_gather | solution.py:16
  487.3 128.1 %all-gather.23.cloned.1.call-start = ((), (), s32[]{:S(2)}) async-start(), calls=%async_computation.7 | async-start | bytes 9437184 | tf_op jit(solution)/shard_map/all_gather | solution.py:16
Sparse Core Ops, SparseCore 0:
  9.5 51.6 all-gather.8
  93.5 49.2 all-gather.10
  172.8 49.0 all-gather.12
  251.5 49.0 all-gather.14
  330.0 49.2 all-gather.16
  408.7 49.1 all-gather.18
  487.4 49.1 all-gather.20
  566.1 49.2 all-gather.22
where the time goes:
time: 657 us; the launch traced here: 655 us
  matrix products  248 us (38%)
  waiting for transfers between devices  189 us (29%)
  blocking collectives  185 us (28%)
  between operations  23.9 us (4%)
    dot_general x8, matrix products, local_sweeps(): prod_rows = jnp.dot(mat_rows, gathered, preferred_element_type=jnp.float32)  238 us
    all_gather x8, waiting for transfers between devices, local_sweeps(): lax.all_gather(rank_rows.astype(jnp.bfloat16), 'row', axis=0, tiled=True)  189 us
    psum x8, blocking collectives, local_sweeps(): lax.psum(jnp.dot(dang_float, rank_rows, preferred_element_type=jnp.float3...  185 us
  transfers between devices with their start and end apart: 8, of which 8 were waited for; matrix products, arithmetic and copies ran while one was open for 2% of the time, Pallas kernels for 0%

commit v1 on v0

v1 whole, which is shorter than its diff:
```python
import functools

import jax
import jax.numpy as jnp
from jax import lax
from jax.experimental import pallas as pl
from jax.experimental.pallas import tpu as pltpu
from jax.sharding import PartitionSpec as P

MESH = pl.DeviceIdType.MESH

DEV = 8
ROWS = 2048
TILE = 512
HALF = 128
COLS = 256
KEEP = 14
RING = 6
CHUNKS = 32
MROWS = 1024

X_SLOTS = ((0, 0, 0), (0, 1, 0), (0, 0, 1), (0, 1, 1), (1, 2, 0), (1, 2, 1), (0, 2, 0), (0, 2, 1), (1, 3, 0), (1, 3, 1), (0, 3, 0), (0, 3, 1))
Y_SLOTS = ((0, 2, 0), (0, 3, 0), (0, 2, 1), (0, 3, 1), (1, 0, 0), (1, 0, 1), (0, 0, 0), (0, 0, 1), (1, 1, 0), (1, 1, 1), (0, 1, 0), (0, 1, 1))


def kernel(sweeps, mat, tele, dang, damp, start, out, rbuf, abuf, acc, tbuf, dcol, draw, mbuf, asem, lsem, ssem, xsem, ysem, dsem, msend, mrecv, osem):
    me = lax.axis_index("row")
    core = lax.rem(me, 2)
    xbit = lax.rem(lax.div(me, 2), 2)
    ybit = lax.div(me, 4)

    def device(xb, yb, cb):
        return yb * 4 + xb * 2 + cb

    xn, yn, pt = device(1 - xbit, ybit, core), device(xbit, 1 - ybit, core), device(xbit, ybit, 1 - core)
    dg = device(1 - xbit, 1 - ybit, core)
    pxn, pyn, pdg = device(1 - xbit, ybit, 1 - core), device(xbit, 1 - ybit, 1 - core), device(1 - xbit, 1 - ybit, 1 - core)

    order = [(me, j) for j in range(4)] + [(pt, j) for j in range(4)]
    order += [(xn, 0), (xn, 1), (yn, 2), (yn, 3), (pxn, 0), (pxn, 1), (pyn, 2), (pyn, 3)]
    order += [(dg, 2), (dg, 0), (pdg, 2), (pdg, 0), (xn, 2), (yn, 0), (pxn, 2), (pyn, 0)]
    order += [(dg, 3), (dg, 1), (pdg, 3), (pdg, 1), (xn, 3), (yn, 1), (pxn, 3), (pyn, 1)]

    def first(dv, j):
        return pl.multiple_of(dv * ROWS + j * TILE, TILE)

    def slot_of(c):
        return c if c < KEEP else KEEP + (c - KEEP) % RING

    def load(c):
        dv, j = order[c]
        return pltpu.make_async_copy(mat.at[:, pl.ds(first(dv, j), TILE)], abuf.at[slot_of(c)], asem.at[slot_of(c)])

    def piece(p, dv, j, h):
        return rbuf.at[p, h, pl.ds(first(dv, j), TILE), :]

    def send(p, dv, j, h, to, recv):
        return pltpu.make_async_remote_copy(
            src_ref=piece(p, dv, j, h), dst_ref=piece(p, dv, j, h), send_sem=ssem.at[p, h], recv_sem=recv,
            device_id={"row": to}, device_id_type=MESH,
        )

    def arrived(p, dv, j, h, recv):
        pltpu.make_async_copy(piece(p, dv, j, h), piece(p, dv, j, h), recv).wait()

    def send_x(p, k):
        fwd, j, h = X_SLOTS[k]
        send(p, yn if fwd else me, j, h, xn, xsem.at[p, k]).start()

    def send_y(p, k):
        fwd, j, h = Y_SLOTS[k]
        send(p, xn if fwd else me, j, h, yn, ysem.at[p, k]).start()

    def share_own(p, j, h):
        send(p, me, j, h, pt, dsem.at[p, 2 * j + h]).start()

    def take(p, k):
        fwd, j, h = X_SLOTS[k]
        src = dg if fwd else xn
        arrived(p, src, j, h, xsem.at[p, k])
        send(p, src, j, h, pt, dsem.at[p, 8 + k]).start()
        fwd, j, h = Y_SLOTS[k]
        src = dg if fwd else yn
        arrived(p, src, j, h, ysem.at[p, k])
        send(p, src, j, h, pt, dsem.at[p, 20 + k]).start()

    def take_shared(p, ks):
        for k in ks:
            fwd, j, h = X_SLOTS[k]
            arrived(p, pdg if fwd else pxn, j, h, dsem.at[p, 8 + k])
            fwd, j, h = Y_SLOTS[k]
            arrived(p, pdg if fwd else pyn, j, h, dsem.at[p, 20 + k])

    def mass_of(values, rows, h):
        weighted = values * dcol[rows, :]
        return jnp.sum(weighted.reshape(-1, 8, HALF), axis=0).sum(axis=0, keepdims=True)

    def send_mass(p):
        for dx, dy, dc in [(a, b, c) for a in range(2) for b in range(2) for c in range(2)][1:]:
            to = device(lax.rem(xbit + dx, 2), lax.rem(ybit + dy, 2), lax.rem(core + dc, 2))
            pltpu.make_async_remote_copy(
                src_ref=mbuf.at[p, me], dst_ref=mbuf.at[p, me], send_sem=msend.at[p], recv_sem=mrecv.at[p],
                device_id={"row": to}, device_id_type=MESH,
            ).start()

    def wait_a(t, cs):
        for c in cs:
            if c < KEEP:
                @pl.when(t == 0)
                def _():
                    load(c).wait()
            else:
                load(c).wait()

    def refill(t, cs):
        for c in cs:
            if c < KEEP:
                continue
            if c + RING < CHUNKS:
                load(c + RING).start()
            else:
                @pl.when(t < sweeps - 1)
                def _():
                    load(c + RING - (CHUNKS - KEEP)).start()

    def wide(p, c):
        r = pl.ds(first(*order[c]), TILE)
        return jnp.concatenate([rbuf[p, 0, r, :], rbuf[p, 1, r, :]], axis=1)

    def matmul(t, p, cs, init=False):
        wait_a(t, cs)

        @pl.loop(0, ROWS // MROWS)
        def _(i):
            rows = pl.ds(pl.multiple_of(i * MROWS, MROWS), MROWS)
            total = None if init else acc[rows, :]
            for c in cs:
                part = jnp.dot(abuf[slot_of(c), rows, :], wide(p, c), preferred_element_type=jnp.float32)
                total = part if total is None else total + part
            acc[rows, :] = total

        refill(t, cs)

    def matmul_half(p, cs, h):
        @pl.loop(0, ROWS // MROWS)
        def _(i):
            rows = pl.ds(pl.multiple_of(i * MROWS, MROWS), MROWS)
            lanes = pl.ds(h * HALF, HALF)
            total = acc[rows, lanes]
            for c in cs:
                total += jnp.dot(abuf[slot_of(c), rows, :], rbuf[p, h, pl.ds(first(*order[c]), TILE), :], preferred_element_type=jnp.float32)
            acc[rows, lanes] = total

    own_rows = pltpu.make_async_copy(start, acc, lsem.at[0])
    own_rows.start()
    own_dang = pltpu.make_async_copy(dang, draw, lsem.at[1])
    own_dang.start()
    for c in range(KEEP):
        load(c).start()
    own_tele = pltpu.make_async_copy(tele, tbuf, lsem.at[2])
    own_tele.start()
    for c in range(KEEP, KEEP + RING):
        load(c).start()

    barrier = pltpu.get_barrier_semaphore()
    for dx, dy, dc in [(a, b, c) for a in range(2) for b in range(2) for c in range(2)][1:]:
        to = device(lax.rem(xbit + dx, 2), lax.rem(ybit + dy, 2), lax.rem(core + dc, 2))
        pl.semaphore_signal(barrier, inc=1, device_id={"row": to}, device_id_type=MESH)
    own_rows.wait()
    for h in range(2):
        for j in range(4):
            rbuf[0, h, pl.ds(first(me, j), TILE), :] = acc[pl.ds(j * TILE, TILE), pl.ds(h * HALF, HALF)].astype(jnp.bfloat16)
    pl.semaphore_wait(barrier, DEV - 1)
    for k in range(4):
        send_x(0, k)
        send_y(0, k)
    for h in range(2):
        for j in range(4):
            share_own(0, j, h)
    own_dang.wait()
    for i in range(ROWS // 128):
        line = jnp.broadcast_to(draw[pl.ds(i, 1), :].astype(jnp.float32), (128, 128))
        dcol[pl.ds(i * 128, 128), :] = jnp.transpose(line)
    for h in range(2):
        total = None
        for j in range(4):
            rows = pl.ds(j * TILE, TILE)
            part = mass_of(acc[rows, pl.ds(h * HALF, HALF)], rows, h)
            total = part if total is None else total + part
        mbuf[0, me, :, pl.ds(h * HALF, HALF)] = total
    send_mass(0)
    own_tele.wait()

    @pl.loop(0, sweeps)
    def _(t):
        p = lax.rem(t, 2)
        q = 1 - p
        matmul(t, p, range(0, 4), init=True)
        take(p, 0)
        send_x(p, 4)
        send_y(p, 4)
        for j in range(4):
            for h in range(2):
                arrived(p, pt, j, h, dsem.at[p, 2 * j + h])
        matmul(t, p, range(4, 8))
        take(p, 1)
        take(p, 2)
        for k in (5, 6, 7):
            send_x(p, k)
            send_y(p, k)
        take(p, 3)
        for k in (8, 9, 10, 11):
            send_x(p, k)
            send_y(p, k)
        matmul(t, p, range(8, 12))
        take_shared(p, range(0, 4))
        matmul(t, p, range(12, 16))
        for s in range(3):
            take(p, 4 + 2 * s)
            take(p, 5 + 2 * s)
            matmul(t, p, range(16 + 4 * s, 18 + 4 * s))
            take_shared(p, (4 + 2 * s, 5 + 2 * s))
            matmul(t, p, range(18 + 4 * s, 20 + 4 * s))
        wait_a(t, range(28, 32))
        pltpu.make_async_copy(mbuf.at[p, pl.ds(0, DEV - 1)], mbuf.at[p, pl.ds(0, DEV - 1)], mrecv.at[p]).wait()
        pltpu.make_async_copy(mbuf.at[p, pl.ds(0, DEV - 1)], mbuf.at[p, pl.ds(0, DEV - 1)], msend.at[p]).wait()
        mass = jnp.sum(mbuf[p], axis=0)
        factor = damp[t]
        nodes = DEV * ROWS
        for h in range(2):
            take(p, 10 + h)
            matmul_half(p, (28, 29), h)
            take_shared(p, (10 + h,))
            sent = rbuf.at[p, h, pl.ds(0, 28 * TILE), :]
            pltpu.make_async_copy(sent, sent, ssem.at[p, h]).wait()
            lanes = pl.ds(h * HALF, HALF)
            row = (factor / nodes) * mass[:, h * HALF:(h + 1) * HALF]
            held = None
            for j in (0, 2, 1, 3):
                rows = pl.ds(j * TILE, TILE)
                total = acc[rows, lanes]
                for c in (30, 31):
                    total += jnp.dot(abuf[slot_of(c), rows, :], rbuf[p, h, pl.ds(first(*order[c]), TILE), :], preferred_element_type=jnp.float32)
                new = factor * total + (1.0 - factor) * tbuf[rows, lanes] + row
                acc[rows, lanes] = new
                rbuf[q, h, pl.ds(first(me, j), TILE), :] = new.astype(jnp.bfloat16)
                part = mass_of(new, rows, h)
                held = part if held is None else held + part

                @pl.when(t < sweeps - 1)
                def _():
                    if j in (0, 1):
                        send_x(q, j + 2 * h)
                    else:
                        send_y(q, j - 2 + 2 * h)
                    share_own(q, j, h)

                if h == 1:
                    @pl.when(t == sweeps - 1)
                    def _():
                        pltpu.make_async_copy(acc.at[rows, :], out.at[rows, :], osem.at[j]).start()
            mbuf[q, me, :, lanes] = held
        refill(t, range(28, 32))

        @pl.when(t < sweeps - 1)
        def _():
            send_mass(q)

    for j in range(4):
        rows = pl.ds(j * TILE, TILE)
        pltpu.make_async_copy(acc.at[rows, :], out.at[rows, :], osem.at[j]).wait()


def solution(mesh):
    spec_rows = P(("batch", "row"), None)
    spec_vec = P(("batch", "row"))

    def local_sweeps(mat_rows, tele_rows, dang_rows, damping, start_rows):
        sweeps = damping.shape[0]
        hbm = pl.BlockSpec(memory_space=pl.ANY)
        return pl.pallas_call(
            functools.partial(kernel, sweeps),
            out_shape=jax.ShapeDtypeStruct((ROWS, COLS), jnp.float32),
            in_specs=[hbm, hbm, hbm, pl.BlockSpec(memory_space=pltpu.SMEM), hbm],
            out_specs=hbm,
            scratch_shapes=[
                pltpu.VMEM((2, 2, DEV * ROWS, HALF), jnp.bfloat16),
                pltpu.VMEM((KEEP + RING, ROWS, TILE), jnp.bfloat16),
                pltpu.VMEM((ROWS, COLS), jnp.float32),
                pltpu.VMEM((ROWS, COLS), jnp.float32),
                pltpu.VMEM((ROWS, HALF), jnp.float32),
                pltpu.VMEM((ROWS // 128, 128), jnp.int32),
                pltpu.VMEM((2, DEV, 1, COLS), jnp.float32),
                pltpu.SemaphoreType.DMA((KEEP + RING,)),
                pltpu.SemaphoreType.DMA((3,)),
                pltpu.SemaphoreType.DMA((2, 2)),
                pltpu.SemaphoreType.DMA((2, 12)),
                pltpu.SemaphoreType.DMA((2, 12)),
                pltpu.SemaphoreType.DMA((2, 32)),
                pltpu.SemaphoreType.DMA((2,)),
                pltpu.SemaphoreType.DMA((2,)),
                pltpu.SemaphoreType.DMA((4,)),
            ],
            compiler_params=pltpu.CompilerParams(collective_id=0, has_side_effects=True, vmem_limit_bytes=67043328),
            name="sweeps",
        )(mat_rows, tele_rows, dang_rows.reshape(ROWS // 128, 128), damping, start_rows)

    return jax.shard_map(local_sweeps, mesh=mesh, in_specs=(spec_rows, spec_rows, spec_vec, P(None), spec_rows), out_specs=spec_rows, check_vma=False)
```

time: 657 us -> 325 us (0.49)
  Pallas kernels: 0 us -> 321 us
  matrix products: 248 us -> 0 us
  waiting for transfers between devices: 189 us -> 0 us
  blocking collectives: 185 us -> 0 us
  between operations: 23.9 us -> 0.01 us
    pallas_call x0 -> x1, Pallas kernels: none -> 321 us  [local_sweeps(): pl.pallas_call(functools.partial(kernel, sweeps), out_shape=jax.ShapeDtyp...]
    dot_general x16 -> x0, matrix products: 248 us -> none  [the longest x8 238 us: local_sweeps(): prod_rows = jnp.dot(mat_rows, gathered, preferred_element_type=jnp.float32)]
    all_gather x8 -> x0, waiting for transfers between devices: 189 us -> none  [local_sweeps(): lax.all_gather(rank_rows.astype(jnp.bfloat16), 'row', axis=0, tiled=True)]
    psum x8 -> x0, blocking collectives: 185 us -> none  [local_sweeps(): lax.psum(jnp.dot(dang_float, rank_rows, preferred_element_type=jnp.float3...]
  transfers between devices with their start and end apart: 8 -> 0, of which waited for: 8 -> 0; matrix products, arithmetic and copies ran while one was open for 2% -> 0% of each run, Pallas kernels for 0% -> 0%
where the time goes in v1:
time: 325 us; the launch traced here: 324 us
  Pallas kernels  321 us (99%)
    pallas_call x1, Pallas kernels, local_sweeps(): pl.pallas_call(functools.partial(kernel, sweeps), out_shape=jax.ShapeDtyp...  321 us

profile of v1, /device:TPU:0, one launch (start us, length us, event | category | flops | bytes accessed | tf_op | source)
XLA Modules:
  0.0 324.5 jit_solution(6208780598584728568)
XLA Ops:
  0.0 321.4 %sweeps.1 = f32[2048,256]{1,0:T(8,128)} custom-call(bf16[2048,16384]{1,0:T(8,128)(2,1)} %mat.1, f32[2048,256]{1,0:T(8,128)} %tele.1, s32[16,128]{1,0:T(8,128)} %bitcast.1, f32[8]{0:T(128)} %damp.1, f32[2048,256]{1,0:T(8,128)} %start.1), custom_call_target="tpu_custom_call" | custom-call | tf_op jit(solution)/shard_map/sweeps/pallas_call | solution.py:281
  321.4 3.0 copy.7

commit v2 on v1

--- a/solution.py
+++ b/solution.py
@@ -14,16 +14,16 @@
 TILE = 512
 HALF = 128
 COLS = 256
-KEEP = 14
+KEPT = (0, 1, 2, 3, 14, 15, 24, 25, 26, 27, 28, 29, 30, 31)
+STREAMED = tuple(c for c in range(32) if c not in KEPT)
 RING = 6
-CHUNKS = 32
 MROWS = 1024
 
-X_SLOTS = ((0, 0, 0), (0, 1, 0), (0, 0, 1), (0, 1, 1), (1, 2, 0), (1, 2, 1), (0, 2, 0), (0, 2, 1), (1, 3, 0), (1, 3, 1), (0, 3, 0), (0, 3, 1))
-Y_SLOTS = ((0, 2, 0), (0, 3, 0), (0, 2, 1), (0, 3, 1), (1, 0, 0), (1, 0, 1), (0, 0, 0), (0, 0, 1), (1, 1, 0), (1, 1, 1), (0, 1, 0), (0, 1, 1))
-
-
-def kernel(sweeps, mat, tele, dang, damp, start, out, rbuf, abuf, acc, tbuf, dcol, draw, mbuf, asem, lsem, ssem, xsem, ysem, dsem, msend, mrecv, osem):
+X_SLOTS = ((0, 0, 0), (0, 1, 0), (0, 0, 1), (0, 1, 1), (1, 2, 0), (1, 2, 1), (0, 2, 0), (0, 2, 1), (1, 3, 0), (0, 3, 0), (1, 3, 1), (0, 3, 1))
+Y_SLOTS = ((0, 2, 0), (0, 3, 0), (0, 2, 1), (0, 3, 1), (1, 0, 0), (1, 0, 1), (0, 0, 0), (0, 0, 1), (1, 1, 0), (0, 1, 0), (1, 1, 1), (0, 1, 1))
+
+
+def kernel(sweeps, mat, tele, dang, damp, start, out, factors, rbuf, abuf, acc, tbuf, dcol, draw, mbuf, asem, lsem, ssem, xsem, ysem, dsem, msend, mrecv, osem):
     me = lax.axis_index("row")
     core = lax.rem(me, 2)
     xbit = lax.rem(lax.div(me, 2), 2)
@@ -45,7 +45,7 @@
         return pl.multiple_of(dv * ROWS + j * TILE, TILE)
 
     def slot_of(c):
-        return c if c < KEEP else KEEP + (c - KEEP) % RING
+        return KEPT.index(c) if c in KEPT else len(KEPT) + STREAMED.index(c) % RING
 
     def load(c):
         dv, j = order[c]
@@ -105,7 +105,7 @@
 
     def wait_a(t, cs):
         for c in cs:
-            if c < KEEP:
+            if c in KEPT:
                 @pl.when(t == 0)
                 def _():
                     load(c).wait()
@@ -114,14 +114,15 @@
 
     def refill(t, cs):
         for c in cs:
-            if c < KEEP:
+            if c in KEPT:
                 continue
-            if c + RING < CHUNKS:
-                load(c + RING).start()
+            later = STREAMED.index(c) + RING
+            if later < len(STREAMED):
+                load(STREAMED[later]).start()
             else:
                 @pl.when(t < sweeps - 1)
                 def _():
-                    load(c + RING - (CHUNKS - KEEP)).start()
+                    load(STREAMED[later - len(STREAMED)]).start()
 
     def wide(p, c):
         r = pl.ds(first(*order[c]), TILE)
@@ -155,12 +156,12 @@
     own_rows.start()
     own_dang = pltpu.make_async_copy(dang, draw, lsem.at[1])
     own_dang.start()
-    for c in range(KEEP):
+    own_damp = pltpu.make_async_copy(damp, factors, lsem.at[3])
+    own_damp.start()
+    for c in sorted(KEPT + STREAMED[:RING]):
         load(c).start()
     own_tele = pltpu.make_async_copy(tele, tbuf, lsem.at[2])
     own_tele.start()
-    for c in range(KEEP, KEEP + RING):
-        load(c).start()
 
     barrier = pltpu.get_barrier_semaphore()
     for dx, dy, dc in [(a, b, c) for a in range(2) for b in range(2) for c in range(2)][1:]:
@@ -190,6 +191,7 @@
         mbuf[0, me, :, pl.ds(h * HALF, HALF)] = total
     send_mass(0)
     own_tele.wait()
+    own_damp.wait()
 
     @pl.loop(0, sweeps)
     def _(t):
@@ -215,22 +217,26 @@
         matmul(t, p, range(8, 12))
         take_shared(p, range(0, 4))
         matmul(t, p, range(12, 16))
-        for s in range(3):
+        for s in range(2):
             take(p, 4 + 2 * s)
             take(p, 5 + 2 * s)
             matmul(t, p, range(16 + 4 * s, 18 + 4 * s))
             take_shared(p, (4 + 2 * s, 5 + 2 * s))
             matmul(t, p, range(18 + 4 * s, 20 + 4 * s))
-        wait_a(t, range(28, 32))
+        wait_a(t, range(24, 32))
         pltpu.make_async_copy(mbuf.at[p, pl.ds(0, DEV - 1)], mbuf.at[p, pl.ds(0, DEV - 1)], mrecv.at[p]).wait()
         pltpu.make_async_copy(mbuf.at[p, pl.ds(0, DEV - 1)], mbuf.at[p, pl.ds(0, DEV - 1)], msend.at[p]).wait()
         mass = jnp.sum(mbuf[p], axis=0)
-        factor = damp[t]
+        factor = factors[t]
         nodes = DEV * ROWS
         for h in range(2):
-            take(p, 10 + h)
+            take(p, 8 + 2 * h)
+            matmul_half(p, (24, 25), h)
+            take_shared(p, (8 + 2 * h,))
+            matmul_half(p, (26, 27), h)
+            take(p, 9 + 2 * h)
             matmul_half(p, (28, 29), h)
-            take_shared(p, (10 + h,))
+            take_shared(p, (9 + 2 * h,))
             sent = rbuf.at[p, h, pl.ds(0, 28 * TILE), :]
             pltpu.make_async_copy(sent, sent, ssem.at[p, h]).wait()
             lanes = pl.ds(h * HALF, HALF)
@@ -255,20 +261,19 @@
                         send_y(q, j - 2 + 2 * h)
                     share_own(q, j, h)
 
-                if h == 1:
-                    @pl.when(t == sweeps - 1)
-                    def _():
-                        pltpu.make_async_copy(acc.at[rows, :], out.at[rows, :], osem.at[j]).start()
+                @pl.when(t == sweeps - 1)
+                def _():
+                    pltpu.make_async_copy(acc.at[rows, lanes], out.at[rows, lanes], osem.at[h, j]).start()
             mbuf[q, me, :, lanes] = held
-        refill(t, range(28, 32))
 
         @pl.when(t < sweeps - 1)
         def _():
             send_mass(q)
 
-    for j in range(4):
-        rows = pl.ds(j * TILE, TILE)
-        pltpu.make_async_copy(acc.at[rows, :], out.at[rows, :], osem.at[j]).wait()
+    for h in range(2):
+        for j in range(4):
+            part = (pl.ds(j * TILE, TILE), pl.ds(h * HALF, HALF))
+            pltpu.make_async_copy(acc.at[part], out.at[part], osem.at[h, j]).wait()
 
 
 def solution(mesh):
@@ -281,25 +286,26 @@
         return pl.pallas_call(
             functools.partial(kernel, sweeps),
             out_shape=jax.ShapeDtypeStruct((ROWS, COLS), jnp.float32),
-            in_specs=[hbm, hbm, hbm, pl.BlockSpec(memory_space=pltpu.SMEM), hbm],
+            in_specs=[hbm] * 5,
             out_specs=hbm,
             scratch_shapes=[
+                pltpu.SMEM((sweeps,), jnp.float32),
                 pltpu.VMEM((2, 2, DEV * ROWS, HALF), jnp.bfloat16),
-                pltpu.VMEM((KEEP + RING, ROWS, TILE), jnp.bfloat16),
+                pltpu.VMEM((len(KEPT) + RING, ROWS, TILE), jnp.bfloat16),
                 pltpu.VMEM((ROWS, COLS), jnp.float32),
                 pltpu.VMEM((ROWS, COLS), jnp.float32),
                 pltpu.VMEM((ROWS, HALF), jnp.float32),
                 pltpu.VMEM((ROWS // 128, 128), jnp.int32),
                 pltpu.VMEM((2, DEV, 1, COLS), jnp.float32),
-                pltpu.SemaphoreType.DMA((KEEP + RING,)),
-                pltpu.SemaphoreType.DMA((3,)),
+                pltpu.SemaphoreType.DMA((len(KEPT) + RING,)),
+                pltpu.SemaphoreType.DMA((4,)),
                 pltpu.SemaphoreType.DMA((2, 2)),
                 pltpu.SemaphoreType.DMA((2, 12)),
                 pltpu.SemaphoreType.DMA((2, 12)),
                 pltpu.SemaphoreType.DMA((2, 32)),
                 pltpu.SemaphoreType.DMA((2,)),
                 pltpu.SemaphoreType.DMA((2,)),
-                pltpu.SemaphoreType.DMA((4,)),
+                pltpu.SemaphoreType.DMA((2, 4)),
             ],
             compiler_params=pltpu.CompilerParams(collective_id=0, has_side_effects=True, vmem_limit_bytes=67043328),
             name="sweeps",

time: 325 us -> 307 us (0.945)
  Pallas kernels: 321 us -> 304 us
    pallas_call x1, Pallas kernels: 321 us -> 304 us  [local_sweeps(): pl.pallas_call(functools.partial(kernel, sweeps), out_shape=jax.ShapeDtyp...]
where the time goes in v2:
time: 307 us
  Pallas kernels  304 us (99%)
    pallas_call x1, Pallas kernels, local_sweeps(): pl.pallas_call(functools.partial(kernel, sweeps), out_shape=jax.ShapeDtyp...  304 us

profile of v2, /device:TPU:0, one launch (start us, length us, event | category | flops | bytes accessed | tf_op | source)
XLA Modules:
  0.0 307.3 jit_solution(8200841571059497442)
XLA Ops:
  0.0 304.2 %sweeps.1 = f32[2048,256]{1,0:T(8,128)} custom-call(bf16[2048,16384]{1,0:T(8,128)(2,1)} %mat.1, f32[2048,256]{1,0:T(8,128)} %tele.1, s32[16,128]{1,0:T(8,128)} %bitcast.1, f32[8]{0:T(128)} %damp.1, f32[2048,256]{1,0:T(8,128)} %start.1), custom_call_target="tpu_custom_call" | custom-call | tf_op jit(solution)/shard_map/sweeps/pallas_call | solution.py:286
  304.2 3.0 copy.7

commit v3 on v2

--- a/solution.py
+++ b/solution.py
@@ -19,8 +19,8 @@
 RING = 6
 MROWS = 1024
 
-X_SLOTS = ((0, 0, 0), (0, 1, 0), (0, 0, 1), (0, 1, 1), (1, 2, 0), (1, 2, 1), (0, 2, 0), (0, 2, 1), (1, 3, 0), (0, 3, 0), (1, 3, 1), (0, 3, 1))
-Y_SLOTS = ((0, 2, 0), (0, 3, 0), (0, 2, 1), (0, 3, 1), (1, 0, 0), (1, 0, 1), (0, 0, 0), (0, 0, 1), (1, 1, 0), (0, 1, 0), (1, 1, 1), (0, 1, 1))
+X_SLOTS = ((0, 0, 0), (0, 2, 0), (0, 0, 1), (0, 2, 1), (0, 1, 0), (0, 1, 1), (1, 1, 0), (1, 1, 1), (1, 3, 0), (0, 3, 0), (1, 3, 1), (0, 3, 1))
+Y_SLOTS = ((0, 1, 0), (0, 3, 0), (0, 1, 1), (0, 3, 1), (0, 0, 0), (0, 0, 1), (1, 0, 0), (1, 0, 1), (1, 2, 0), (0, 2, 0), (1, 2, 1), (0, 2, 1))
 
 
 def kernel(sweeps, mat, tele, dang, damp, start, out, factors, rbuf, abuf, acc, tbuf, dcol, draw, mbuf, asem, lsem, ssem, xsem, ysem, dsem, msend, mrecv, osem):
@@ -37,9 +37,9 @@
     pxn, pyn, pdg = device(1 - xbit, ybit, 1 - core), device(xbit, 1 - ybit, 1 - core), device(1 - xbit, 1 - ybit, 1 - core)
 
     order = [(me, j) for j in range(4)] + [(pt, j) for j in range(4)]
-    order += [(xn, 0), (xn, 1), (yn, 2), (yn, 3), (pxn, 0), (pxn, 1), (pyn, 2), (pyn, 3)]
-    order += [(dg, 2), (dg, 0), (pdg, 2), (pdg, 0), (xn, 2), (yn, 0), (pxn, 2), (pyn, 0)]
-    order += [(dg, 3), (dg, 1), (pdg, 3), (pdg, 1), (xn, 3), (yn, 1), (pxn, 3), (pyn, 1)]
+    order += [(xn, 0), (xn, 2), (yn, 1), (yn, 3), (pxn, 0), (pxn, 2), (pyn, 1), (pyn, 3)]
+    order += [(xn, 1), (yn, 0), (pxn, 1), (pyn, 0), (dg, 1), (dg, 0), (pdg, 1), (pdg, 0)]
+    order += [(dg, 3), (dg, 2), (pdg, 3), (pdg, 2), (xn, 3), (yn, 2), (pxn, 3), (pyn, 2)]
 
     def first(dv, j):
         return pl.multiple_of(dv * ROWS + j * TILE, TILE)
@@ -131,9 +131,8 @@
     def matmul(t, p, cs, init=False):
         wait_a(t, cs)
 
-        @pl.loop(0, ROWS // MROWS)
-        def _(i):
-            rows = pl.ds(pl.multiple_of(i * MROWS, MROWS), MROWS)
+        for i in range(ROWS // MROWS):
+            rows = pl.ds(i * MROWS, MROWS)
             total = None if init else acc[rows, :]
             for c in cs:
                 part = jnp.dot(abuf[slot_of(c), rows, :], wide(p, c), preferred_element_type=jnp.float32)
@@ -143,36 +142,40 @@
         refill(t, cs)
 
     def matmul_half(p, cs, h):
-        @pl.loop(0, ROWS // MROWS)
-        def _(i):
-            rows = pl.ds(pl.multiple_of(i * MROWS, MROWS), MROWS)
+        for i in range(ROWS // MROWS):
+            rows = pl.ds(i * MROWS, MROWS)
             lanes = pl.ds(h * HALF, HALF)
             total = acc[rows, lanes]
             for c in cs:
                 total += jnp.dot(abuf[slot_of(c), rows, :], rbuf[p, h, pl.ds(first(*order[c]), TILE), :], preferred_element_type=jnp.float32)
             acc[rows, lanes] = total
 
-    own_rows = pltpu.make_async_copy(start, acc, lsem.at[0])
-    own_rows.start()
-    own_dang = pltpu.make_async_copy(dang, draw, lsem.at[1])
+    barrier = pltpu.get_barrier_semaphore()
+    for dx, dy, dc in [(a, b, c) for a in range(2) for b in range(2) for c in range(2)][1:]:
+        to = device(lax.rem(xbit + dx, 2), lax.rem(ybit + dy, 2), lax.rem(core + dc, 2))
+        pl.semaphore_signal(barrier, inc=1, device_id={"row": to}, device_id_type=MESH)
+    own_rows = []
+    for j in range(4):
+        rows = pl.ds(j * TILE, TILE)
+        own_rows.append(pltpu.make_async_copy(start.at[rows, :], acc.at[rows, :], lsem.at[3 + j]))
+        own_rows[j].start()
+    own_dang = pltpu.make_async_copy(dang, draw, lsem.at[0])
     own_dang.start()
-    own_damp = pltpu.make_async_copy(damp, factors, lsem.at[3])
+    own_damp = pltpu.make_async_copy(damp, factors, lsem.at[1])
     own_damp.start()
     for c in sorted(KEPT + STREAMED[:RING]):
         load(c).start()
     own_tele = pltpu.make_async_copy(tele, tbuf, lsem.at[2])
     own_tele.start()
-
-    barrier = pltpu.get_barrier_semaphore()
-    for dx, dy, dc in [(a, b, c) for a in range(2) for b in range(2) for c in range(2)][1:]:
-        to = device(lax.rem(xbit + dx, 2), lax.rem(ybit + dy, 2), lax.rem(core + dc, 2))
-        pl.semaphore_signal(barrier, inc=1, device_id={"row": to}, device_id_type=MESH)
-    own_rows.wait()
-    for h in range(2):
-        for j in range(4):
+    for j in range(4):
+        own_rows[j].wait()
+        for h in range(2):
             rbuf[0, h, pl.ds(first(me, j), TILE), :] = acc[pl.ds(j * TILE, TILE), pl.ds(h * HALF, HALF)].astype(jnp.bfloat16)
-    pl.semaphore_wait(barrier, DEV - 1)
-    for k in range(4):
+        if j == 1:
+            pl.semaphore_wait(barrier, DEV - 1)
+            send_x(0, 0)
+            send_y(0, 0)
+    for k in range(1, 6):
         send_x(0, k)
         send_y(0, k)
     for h in range(2):
@@ -197,21 +200,17 @@
     def _(t):
         p = lax.rem(t, 2)
         q = 1 - p
-        matmul(t, p, range(0, 4), init=True)
-        take(p, 0)
-        send_x(p, 4)
-        send_y(p, 4)
         for j in range(4):
             for h in range(2):
                 arrived(p, pt, j, h, dsem.at[p, 2 * j + h])
-        matmul(t, p, range(4, 8))
-        take(p, 1)
-        take(p, 2)
-        for k in (5, 6, 7):
+        matmul(t, p, range(0, 8), init=True)
+        for k in range(3):
+            take(p, k)
+        for k in (6, 7, 8, 9):
             send_x(p, k)
             send_y(p, k)
         take(p, 3)
-        for k in (8, 9, 10, 11):
+        for k in (10, 11):
             send_x(p, k)
             send_y(p, k)
         matmul(t, p, range(8, 12))
@@ -242,28 +241,32 @@
             lanes = pl.ds(h * HALF, HALF)
             row = (factor / nodes) * mass[:, h * HALF:(h + 1) * HALF]
             held = None
-            for j in (0, 2, 1, 3):
-                rows = pl.ds(j * TILE, TILE)
+            for i in range(ROWS // MROWS):
+                rows = pl.ds(i * MROWS, MROWS)
                 total = acc[rows, lanes]
                 for c in (30, 31):
                     total += jnp.dot(abuf[slot_of(c), rows, :], rbuf[p, h, pl.ds(first(*order[c]), TILE), :], preferred_element_type=jnp.float32)
                 new = factor * total + (1.0 - factor) * tbuf[rows, lanes] + row
                 acc[rows, lanes] = new
-                rbuf[q, h, pl.ds(first(me, j), TILE), :] = new.astype(jnp.bfloat16)
+                rbuf[q, h, pl.ds(first(me, 2 * i), MROWS), :] = new.astype(jnp.bfloat16)
                 part = mass_of(new, rows, h)
                 held = part if held is None else held + part
 
                 @pl.when(t < sweeps - 1)
                 def _():
-                    if j in (0, 1):
-                        send_x(q, j + 2 * h)
-                    else:
-                        send_y(q, j - 2 + 2 * h)
-                    share_own(q, j, h)
+                    send_x(q, i + 2 * h)
+                    send_y(q, i + 2 * h)
+                    share_own(q, 2 * i, h)
+                    share_own(q, 2 * i + 1, h)
+                    if i + h == 2:
+                        for k in (4, 5):
+                            send_x(q, k)
+                            send_y(q, k)
 
                 @pl.when(t == sweeps - 1)
                 def _():
-                    pltpu.make_async_copy(acc.at[rows, lanes], out.at[rows, lanes], osem.at[h, j]).start()
+                    pltpu.make_async_copy(acc.at[rows, lanes], out.at[rows, lanes], osem.at[h, i]).start()
+
             mbuf[q, me, :, lanes] = held
 
         @pl.when(t < sweeps - 1)
@@ -271,9 +274,9 @@
             send_mass(q)
 
     for h in range(2):
-        for j in range(4):
-            part = (pl.ds(j * TILE, TILE), pl.ds(h * HALF, HALF))
-            pltpu.make_async_copy(acc.at[part], out.at[part], osem.at[h, j]).wait()
+        for i in range(ROWS // MROWS):
+            part = (pl.ds(i * MROWS, MROWS), pl.ds(h * HALF, HALF))
+            pltpu.make_async_copy(acc.at[part], out.at[part], osem.at[h, i]).wait()
 
 
 def solution(mesh):
@@ -298,14 +301,14 @@
                 pltpu.VMEM((ROWS // 128, 128), jnp.int32),
                 pltpu.VMEM((2, DEV, 1, COLS), jnp.float32),
                 pltpu.SemaphoreType.DMA((len(KEPT) + RING,)),
-                pltpu.SemaphoreType.DMA((4,)),
+                pltpu.SemaphoreType.DMA((7,)),
                 pltpu.SemaphoreType.DMA((2, 2)),
                 pltpu.SemaphoreType.DMA((2, 12)),
                 pltpu.SemaphoreType.DMA((2, 12)),
                 pltpu.SemaphoreType.DMA((2, 32)),
                 pltpu.SemaphoreType.DMA((2,)),
                 pltpu.SemaphoreType.DMA((2,)),
-                pltpu.SemaphoreType.DMA((2, 4)),
+                pltpu.SemaphoreType.DMA((2, 2)),
             ],
             compiler_params=pltpu.CompilerParams(collective_id=0, has_side_effects=True, vmem_limit_bytes=67043328),
             name="sweeps",

time: 307 us -> 295 us (0.961)
  Pallas kernels: 304 us -> 292 us
    pallas_call x1, Pallas kernels: 304 us -> 292 us  [local_sweeps(): pl.pallas_call(functools.partial(kernel, sweeps), out_shape=jax.ShapeDtyp...]
where the time goes in v3:
time: 295 us
  Pallas kernels  292 us (99%)
  local copies, waits for them, and re-layouts  3.05 us (1%)
    pallas_call x1, Pallas kernels, local_sweeps(): pl.pallas_call(functools.partial(kernel, sweeps), out_shape=jax.ShapeDtyp...  292 us

profile of v3, /device:TPU:0, one launch (start us, length us, event | category | flops | bytes accessed | tf_op | source)
XLA Modules:
  0.0 294.6 jit_solution(16071546787337020722)
XLA Ops:
  0.0 291.5 %sweeps.1 = f32[2048,256]{1,0:T(8,128)} custom-call(bf16[2048,16384]{1,0:T(8,128)(2,1)} %mat.1, f32[2048,256]{1,0:T(8,128)} %tele.1, s32[16,128]{1,0:T(8,128)} %bitcast.1, f32[8]{0:T(128)} %damp.1, f32[2048,256]{1,0:T(8,128)} %start.1), custom_call_target="tpu_custom_call" | custom-call | tf_op jit(solution)/shard_map/sweeps/pallas_call | solution.py:289
  291.5 3.0 %copy.7 = f32[2048,256]{1,0:T(8,128)} copy(f32[2048,256]{1,0:T(8,128)} %sweeps.1) | data formatting | bytes 4194304

commit v4 on v3

--- a/solution.py
+++ b/solution.py
@@ -17,13 +17,14 @@
 KEPT = (0, 1, 2, 3, 14, 15, 24, 25, 26, 27, 28, 29, 30, 31)
 STREAMED = tuple(c for c in range(32) if c not in KEPT)
 RING = 6
-MROWS = 1024
+MROWS = 512
+SENT = 1024
 
 X_SLOTS = ((0, 0, 0), (0, 2, 0), (0, 0, 1), (0, 2, 1), (0, 1, 0), (0, 1, 1), (1, 1, 0), (1, 1, 1), (1, 3, 0), (0, 3, 0), (1, 3, 1), (0, 3, 1))
 Y_SLOTS = ((0, 1, 0), (0, 3, 0), (0, 1, 1), (0, 3, 1), (0, 0, 0), (0, 0, 1), (1, 0, 0), (1, 0, 1), (1, 2, 0), (0, 2, 0), (1, 2, 1), (0, 2, 1))
 
 
-def kernel(sweeps, mat, tele, dang, damp, start, out, factors, rbuf, abuf, acc, tbuf, dcol, draw, mbuf, asem, lsem, ssem, xsem, ysem, dsem, msend, mrecv, osem):
+def kernel(sweeps, mat, tele, dang, damp, start, acc, factors, rbuf, abuf, tbuf, dcol, draw, mbuf, asem, lsem, ssem, xsem, ysem, dsem, msend, mrecv):
     me = lax.axis_index("row")
     core = lax.rem(me, 2)
     xbit = lax.rem(lax.div(me, 2), 2)
@@ -92,7 +93,7 @@
             arrived(p, pdg if fwd else pyn, j, h, dsem.at[p, 20 + k])
 
     def mass_of(values, rows, h):
-        weighted = values * dcol[rows, :]
+        weighted = values * dcol[rows, :].astype(jnp.float32)
         return jnp.sum(weighted.reshape(-1, 8, HALF), axis=0).sum(axis=0, keepdims=True)
 
     def send_mass(p):
@@ -184,7 +185,7 @@
     own_dang.wait()
     for i in range(ROWS // 128):
         line = jnp.broadcast_to(draw[pl.ds(i, 1), :].astype(jnp.float32), (128, 128))
-        dcol[pl.ds(i * 128, 128), :] = jnp.transpose(line)
+        dcol[pl.ds(i * 128, 128), :] = jnp.transpose(line).astype(jnp.bfloat16)
     for h in range(2):
         total = None
         for j in range(4):
@@ -241,16 +242,18 @@
             lanes = pl.ds(h * HALF, HALF)
             row = (factor / nodes) * mass[:, h * HALF:(h + 1) * HALF]
             held = None
-            for i in range(ROWS // MROWS):
-                rows = pl.ds(i * MROWS, MROWS)
-                total = acc[rows, lanes]
-                for c in (30, 31):
-                    total += jnp.dot(abuf[slot_of(c), rows, :], rbuf[p, h, pl.ds(first(*order[c]), TILE), :], preferred_element_type=jnp.float32)
-                new = factor * total + (1.0 - factor) * tbuf[rows, lanes] + row
-                acc[rows, lanes] = new
-                rbuf[q, h, pl.ds(first(me, 2 * i), MROWS), :] = new.astype(jnp.bfloat16)
-                part = mass_of(new, rows, h)
-                held = part if held is None else held + part
+            for i in range(ROWS // SENT):
+                for u in range(SENT // TILE):
+                    j = i * (SENT // TILE) + u
+                    rows = pl.ds(j * TILE, TILE)
+                    total = acc[rows, lanes]
+                    for c in (30, 31):
+                        total += jnp.dot(abuf[slot_of(c), rows, :], rbuf[p, h, pl.ds(first(*order[c]), TILE), :], preferred_element_type=jnp.float32)
+                    new = factor * total + (1.0 - factor) * tbuf[rows, lanes] + row
+                    acc[rows, lanes] = new
+                    rbuf[q, h, pl.ds(first(me, j), TILE), :] = new.astype(jnp.bfloat16)
+                    part = mass_of(new, rows, h)
+                    held = part if held is None else held + part
 
                 @pl.when(t < sweeps - 1)
                 def _():
@@ -263,20 +266,11 @@
                             send_x(q, k)
                             send_y(q, k)
 
-                @pl.when(t == sweeps - 1)
-                def _():
-                    pltpu.make_async_copy(acc.at[rows, lanes], out.at[rows, lanes], osem.at[h, i]).start()
-
             mbuf[q, me, :, lanes] = held
 
         @pl.when(t < sweeps - 1)
         def _():
             send_mass(q)
-
-    for h in range(2):
-        for i in range(ROWS // MROWS):
-            part = (pl.ds(i * MROWS, MROWS), pl.ds(h * HALF, HALF))
-            pltpu.make_async_copy(acc.at[part], out.at[part], osem.at[h, i]).wait()
 
 
 def solution(mesh):
@@ -288,16 +282,15 @@
         hbm = pl.BlockSpec(memory_space=pl.ANY)
         return pl.pallas_call(
             functools.partial(kernel, sweeps),
-            out_shape=jax.ShapeDtypeStruct((ROWS, COLS), jnp.float32),
+            out_shape=pltpu.VMEM((ROWS, COLS), jnp.float32),
             in_specs=[hbm] * 5,
-            out_specs=hbm,
+            out_specs=pl.BlockSpec(memory_space=pltpu.VMEM),
             scratch_shapes=[
                 pltpu.SMEM((sweeps,), jnp.float32),
                 pltpu.VMEM((2, 2, DEV * ROWS, HALF), jnp.bfloat16),
                 pltpu.VMEM((len(KEPT) + RING, ROWS, TILE), jnp.bfloat16),
                 pltpu.VMEM((ROWS, COLS), jnp.float32),
-                pltpu.VMEM((ROWS, COLS), jnp.float32),
-                pltpu.VMEM((ROWS, HALF), jnp.float32),
+                pltpu.VMEM((ROWS, HALF), jnp.bfloat16),
                 pltpu.VMEM((ROWS // 128, 128), jnp.int32),
                 pltpu.VMEM((2, DEV, 1, COLS), jnp.float32),
                 pltpu.SemaphoreType.DMA((len(KEPT) + RING,)),
@@ -308,9 +301,8 @@
                 pltpu.SemaphoreType.DMA((2, 32)),
                 pltpu.SemaphoreType.DMA((2,)),
                 pltpu.SemaphoreType.DMA((2,)),
-                pltpu.SemaphoreType.DMA((2, 2)),
             ],
-            compiler_params=pltpu.CompilerParams(collective_id=0, has_side_effects=True, vmem_limit_bytes=67043328),
+            compiler_params=pltpu.CompilerParams(collective_id=0, has_side_effects=True, vmem_limit_bytes=64880640),
             name="sweeps",
         )(mat_rows, tele_rows, dang_rows.reshape(ROWS // 128, 128), damping, start_rows)
 

time: 295 us -> 310 us (1.051)
  Pallas kernels: 292 us -> 308 us
    pallas_call x1, Pallas kernels: 292 us -> 308 us  [local_sweeps(): pl.pallas_call(functools.partial(kernel, sweeps), out_shape=pltpu.VMEM((R...]
where the time goes in v4:
time: 310 us
  Pallas kernels  308 us (99%)
    pallas_call x1, Pallas kernels, local_sweeps(): pl.pallas_call(functools.partial(kernel, sweeps), out_shape=pltpu.VMEM((R...  308 us

profile of v4, /device:TPU:0, one launch (start us, length us, event | category | flops | bytes accessed | tf_op | source)
XLA Modules:
  0.0 309.6 jit_solution(7851204674905107108)
XLA Ops:
  0.0 308.3 %sweeps.1 = f32[2048,256]{1,0:T(8,128)S(1)} custom-call(bf16[2048,16384]{1,0:T(8,128)(2,1)} %mat.1, f32[2048,256]{1,0:T(8,128)} %tele.1, s32[16,128]{1,0:T(8,128)} %bitcast.1, f32[8]{0:T(128)} %damp.1, f32[2048,256]{1,0:T(8,128)} %start.1), custom_call_target="tpu_custom_call" | custom-call | tf_op jit(solution)/shard_map/sweeps/pallas_call | solution.py:283
  308.3 1.3 copy.7

commit v5 on v4

--- a/solution.py
+++ b/solution.py
@@ -17,7 +17,7 @@
 KEPT = (0, 1, 2, 3, 14, 15, 24, 25, 26, 27, 28, 29, 30, 31)
 STREAMED = tuple(c for c in range(32) if c not in KEPT)
 RING = 6
-MROWS = 512
+MROWS = 1024
 SENT = 1024
 
 X_SLOTS = ((0, 0, 0), (0, 2, 0), (0, 0, 1), (0, 2, 1), (0, 1, 0), (0, 1, 1), (1, 1, 0), (1, 1, 1), (1, 3, 0), (0, 3, 0), (1, 3, 1), (0, 3, 1))
@@ -134,11 +134,11 @@
 
         for i in range(ROWS // MROWS):
             rows = pl.ds(i * MROWS, MROWS)
-            total = None if init else acc[rows, :]
+            total = None
             for c in cs:
                 part = jnp.dot(abuf[slot_of(c), rows, :], wide(p, c), preferred_element_type=jnp.float32)
                 total = part if total is None else total + part
-            acc[rows, :] = total
+            acc[rows, :] = total if init else acc[rows, :] + total
 
         refill(t, cs)
 
@@ -146,10 +146,11 @@
         for i in range(ROWS // MROWS):
             rows = pl.ds(i * MROWS, MROWS)
             lanes = pl.ds(h * HALF, HALF)
-            total = acc[rows, lanes]
+            total = None
             for c in cs:
-                total += jnp.dot(abuf[slot_of(c), rows, :], rbuf[p, h, pl.ds(first(*order[c]), TILE), :], preferred_element_type=jnp.float32)
-            acc[rows, lanes] = total
+                part = jnp.dot(abuf[slot_of(c), rows, :], rbuf[p, h, pl.ds(first(*order[c]), TILE), :], preferred_element_type=jnp.float32)
+                total = part if total is None else total + part
+            acc[rows, lanes] += total
 
     barrier = pltpu.get_barrier_semaphore()
     for dx, dy, dc in [(a, b, c) for a in range(2) for b in range(2) for c in range(2)][1:]:
@@ -243,15 +244,17 @@
             row = (factor / nodes) * mass[:, h * HALF:(h + 1) * HALF]
             held = None
             for i in range(ROWS // SENT):
-                for u in range(SENT // TILE):
-                    j = i * (SENT // TILE) + u
-                    rows = pl.ds(j * TILE, TILE)
-                    total = acc[rows, lanes]
+                for u in range(1):
+                    j = 2 * i
+                    rows = pl.ds(j * TILE, SENT)
+                    total = None
                     for c in (30, 31):
-                        total += jnp.dot(abuf[slot_of(c), rows, :], rbuf[p, h, pl.ds(first(*order[c]), TILE), :], preferred_element_type=jnp.float32)
+                        part = jnp.dot(abuf[slot_of(c), rows, :], rbuf[p, h, pl.ds(first(*order[c]), TILE), :], preferred_element_type=jnp.float32)
+                        total = part if total is None else total + part
+                    total += acc[rows, lanes]
                     new = factor * total + (1.0 - factor) * tbuf[rows, lanes] + row
                     acc[rows, lanes] = new
-                    rbuf[q, h, pl.ds(first(me, j), TILE), :] = new.astype(jnp.bfloat16)
+                    rbuf[q, h, pl.ds(first(me, j), SENT), :] = new.astype(jnp.bfloat16)
                     part = mass_of(new, rows, h)
                     held = part if held is None else held + part
 

time: 310 us -> 295 us (0.952)
  Pallas kernels: 308 us -> 294 us
    pallas_call x1, Pallas kernels: 308 us -> 294 us  [local_sweeps(): pl.pallas_call(functools.partial(kernel, sweeps), out_shape=pltpu.VMEM((R...]
where the time goes in v5:
time: 295 us
  Pallas kernels  294 us (100%)
    pallas_call x1, Pallas kernels, local_sweeps(): pl.pallas_call(functools.partial(kernel, sweeps), out_shape=pltpu.VMEM((R...  294 us

profile of v5, /device:TPU:0, one launch (start us, length us, event | category | flops | bytes accessed | tf_op | source)
XLA Modules:
  0.0 295.1 jit_solution(12286590307872630237)
XLA Ops:
  0.0 293.8 %sweeps.1 = f32[2048,256]{1,0:T(8,128)S(1)} custom-call(bf16[2048,16384]{1,0:T(8,128)(2,1)} %mat.1, f32[2048,256]{1,0:T(8,128)} %tele.1, s32[16,128]{1,0:T(8,128)} %bitcast.1, f32[8]{0:T(128)} %damp.1, f32[2048,256]{1,0:T(8,128)} %start.1), custom_call_target="tpu_custom_call" | custom-call | tf_op jit(solution)/shard_map/sweeps/pallas_call | solution.py:286
  293.8 1.3 copy.7

commit v6 on v5

--- a/solution.py
+++ b/solution.py
@@ -238,25 +238,22 @@
             take(p, 9 + 2 * h)
             matmul_half(p, (28, 29), h)
             take_shared(p, (9 + 2 * h,))
-            sent = rbuf.at[p, h, pl.ds(0, 28 * TILE), :]
-            pltpu.make_async_copy(sent, sent, ssem.at[p, h]).wait()
             lanes = pl.ds(h * HALF, HALF)
             row = (factor / nodes) * mass[:, h * HALF:(h + 1) * HALF]
-            held = None
             for i in range(ROWS // SENT):
-                for u in range(1):
-                    j = 2 * i
-                    rows = pl.ds(j * TILE, SENT)
-                    total = None
-                    for c in (30, 31):
-                        part = jnp.dot(abuf[slot_of(c), rows, :], rbuf[p, h, pl.ds(first(*order[c]), TILE), :], preferred_element_type=jnp.float32)
-                        total = part if total is None else total + part
-                    total += acc[rows, lanes]
-                    new = factor * total + (1.0 - factor) * tbuf[rows, lanes] + row
-                    acc[rows, lanes] = new
-                    rbuf[q, h, pl.ds(first(me, j), SENT), :] = new.astype(jnp.bfloat16)
-                    part = mass_of(new, rows, h)
-                    held = part if held is None else held + part
+                rows = pl.ds(i * SENT, SENT)
+                total = None
+                for c in (30, 31):
+                    part = jnp.dot(abuf[slot_of(c), rows, :], rbuf[p, h, pl.ds(first(*order[c]), TILE), :], preferred_element_type=jnp.float32)
+                    total = part if total is None else total + part
+                total += acc[rows, lanes]
+                new = factor * total + (1.0 - factor) * tbuf[rows, lanes] + row
+                acc[rows, lanes] = new
+                rbuf[q, h, pl.ds(first(me, 2 * i), SENT), :] = new.astype(jnp.bfloat16)
+
+                if i == ROWS // SENT - 1:
+                    sent = rbuf.at[p, h, pl.ds(0, 28 * TILE), :]
+                    pltpu.make_async_copy(sent, sent, ssem.at[p, h]).wait()
 
                 @pl.when(t < sweeps - 1)
                 def _():
@@ -269,10 +266,17 @@
                             send_x(q, k)
                             send_y(q, k)
 
-            mbuf[q, me, :, lanes] = held
 
         @pl.when(t < sweeps - 1)
         def _():
+            for h in range(2):
+                lanes = pl.ds(h * HALF, HALF)
+                held = None
+                for j in range(4):
+                    rows = pl.ds(j * TILE, TILE)
+                    part = mass_of(acc[rows, lanes], rows, h)
+                    held = part if held is None else held + part
+                mbuf[q, me, :, lanes] = held
             send_mass(q)
 
 

time: 295 us -> 295 us (level)
  no operation moved by 1% of the time
where the time goes in v6:
time: 295 us
  Pallas kernels  294 us (100%)
    pallas_call x1, Pallas kernels, local_sweeps(): pl.pallas_call(functools.partial(kernel, sweeps), out_shape=pltpu.VMEM((R...  294 us

profile of v6, /device:TPU:0, one launch (start us, length us, event | category | flops | bytes accessed | tf_op | source)
XLA Modules:
  0.0 295.0 jit_solution(6660544783108147819)
XLA Ops:
  0.0 293.7 %sweeps.1 = f32[2048,256]{1,0:T(8,128)S(1)} custom-call(bf16[2048,16384]{1,0:T(8,128)(2,1)} %mat.1, f32[2048,256]{1,0:T(8,128)} %tele.1, s32[16,128]{1,0:T(8,128)} %bitcast.1, f32[8]{0:T(128)} %damp.1, f32[2048,256]{1,0:T(8,128)} %start.1), custom_call_target="tpu_custom_call" | custom-call | tf_op jit(solution)/shard_map/sweeps/pallas_call | solution.py:290
  293.7 1.3 copy.7

commit v7 on v6

--- a/solution.py
+++ b/solution.py
@@ -93,8 +93,13 @@
             arrived(p, pdg if fwd else pyn, j, h, dsem.at[p, 20 + k])
 
     def mass_of(values, rows, h):
-        weighted = values * dcol[rows, :].astype(jnp.float32)
-        return jnp.sum(weighted.reshape(-1, 8, HALF), axis=0).sum(axis=0, keepdims=True)
+        total = None
+        for u in range(TILE // 128):
+            line = rows.start // 128 + u
+            part = values[u * 128:(u + 1) * 128] * dcol[:, line:line + 1]
+            part = jnp.sum(part.reshape(-1, 8, HALF), axis=0)
+            total = part if total is None else total + part
+        return jnp.sum(total, axis=0, keepdims=True)
 
     def send_mass(p):
         for dx, dy, dc in [(a, b, c) for a in range(2) for b in range(2) for c in range(2)][1:]:
@@ -184,9 +189,8 @@
         for j in range(4):
             share_own(0, j, h)
     own_dang.wait()
-    for i in range(ROWS // 128):
-        line = jnp.broadcast_to(draw[pl.ds(i, 1), :].astype(jnp.float32), (128, 128))
-        dcol[pl.ds(i * 128, 128), :] = jnp.transpose(line).astype(jnp.bfloat16)
+    lines = jnp.concatenate([draw[...].astype(jnp.float32), jnp.zeros((128 - ROWS // 128, 128), jnp.float32)], axis=0)
+    dcol[...] = jnp.transpose(lines)
     for h in range(2):
         total = None
         for j in range(4):
@@ -241,15 +245,16 @@
             lanes = pl.ds(h * HALF, HALF)
             row = (factor / nodes) * mass[:, h * HALF:(h + 1) * HALF]
             for i in range(ROWS // SENT):
-                rows = pl.ds(i * SENT, SENT)
-                total = None
-                for c in (30, 31):
-                    part = jnp.dot(abuf[slot_of(c), rows, :], rbuf[p, h, pl.ds(first(*order[c]), TILE), :], preferred_element_type=jnp.float32)
-                    total = part if total is None else total + part
-                total += acc[rows, lanes]
-                new = factor * total + (1.0 - factor) * tbuf[rows, lanes] + row
-                acc[rows, lanes] = new
-                rbuf[q, h, pl.ds(first(me, 2 * i), SENT), :] = new.astype(jnp.bfloat16)
+                for j in (2 * i, 2 * i + 1):
+                    rows = pl.ds(j * TILE, TILE)
+                    total = None
+                    for c in (30, 31):
+                        part = jnp.dot(abuf[slot_of(c), rows, :], rbuf[p, h, pl.ds(first(*order[c]), TILE), :], preferred_element_type=jnp.float32)
+                        total = part if total is None else total + part
+                    total += acc[rows, lanes]
+                    new = factor * total + (1.0 - factor) * tbuf[rows, lanes] + row
+                    acc[rows, lanes] = new
+                    rbuf[q, h, pl.ds(first(me, j), TILE), :] = new.astype(jnp.bfloat16)
 
                 if i == ROWS // SENT - 1:
                     sent = rbuf.at[p, h, pl.ds(0, 28 * TILE), :]
@@ -297,7 +302,7 @@
                 pltpu.VMEM((2, 2, DEV * ROWS, HALF), jnp.bfloat16),
                 pltpu.VMEM((len(KEPT) + RING, ROWS, TILE), jnp.bfloat16),
                 pltpu.VMEM((ROWS, COLS), jnp.float32),
-                pltpu.VMEM((ROWS, HALF), jnp.bfloat16),
+                pltpu.VMEM((128, 128), jnp.float32),
                 pltpu.VMEM((ROWS // 128, 128), jnp.int32),
                 pltpu.VMEM((2, DEV, 1, COLS), jnp.float32),
                 pltpu.SemaphoreType.DMA((len(KEPT) + RING,)),
@@ -309,7 +314,7 @@
                 pltpu.SemaphoreType.DMA((2,)),
                 pltpu.SemaphoreType.DMA((2,)),
             ],
-            compiler_params=pltpu.CompilerParams(collective_id=0, has_side_effects=True, vmem_limit_bytes=64880640),
+            compiler_params=pltpu.CompilerParams(collective_id=0, has_side_effects=True, vmem_limit_bytes=64946176),
             name="sweeps",
         )(mat_rows, tele_rows, dang_rows.reshape(ROWS // 128, 128), damping, start_rows)
 

time: 295 us -> 299 us (1.014)
  Pallas kernels: 294 us -> 298 us
    pallas_call x1, Pallas kernels: 294 us -> 298 us  [local_sweeps(): pl.pallas_call(functools.partial(kernel, sweeps), out_shape=pltpu.VMEM((R...]
where the time goes in v7:
time: 299 us
  Pallas kernels  298 us (100%)
    pallas_call x1, Pallas kernels, local_sweeps(): pl.pallas_call(functools.partial(kernel, sweeps), out_shape=pltpu.VMEM((R...  298 us

profile of v7, /device:TPU:0, one launch (start us, length us, event | category | flops | bytes accessed | tf_op | source)
XLA Modules:
  0.0 298.9 jit_solution(9606855983882183787)
XLA Ops:
  0.0 297.5 %sweeps.1 = f32[2048,256]{1,0:T(8,128)S(1)} custom-call(bf16[2048,16384]{1,0:T(8,128)(2,1)} %mat.1, f32[2048,256]{1,0:T(8,128)} %tele.1, s32[16,128]{1,0:T(8,128)} %bitcast.1, f32[8]{0:T(128)} %damp.1, f32[2048,256]{1,0:T(8,128)} %start.1), custom_call_target="tpu_custom_call" | custom-call | tf_op jit(solution)/shard_map/sweeps/pallas_call | solution.py:295
  297.6 1.3 copy.7

commit v8 on v7

--- a/solution.py
+++ b/solution.py
@@ -245,16 +245,11 @@
             lanes = pl.ds(h * HALF, HALF)
             row = (factor / nodes) * mass[:, h * HALF:(h + 1) * HALF]
             for i in range(ROWS // SENT):
-                for j in (2 * i, 2 * i + 1):
-                    rows = pl.ds(j * TILE, TILE)
-                    total = None
-                    for c in (30, 31):
-                        part = jnp.dot(abuf[slot_of(c), rows, :], rbuf[p, h, pl.ds(first(*order[c]), TILE), :], preferred_element_type=jnp.float32)
-                        total = part if total is None else total + part
-                    total += acc[rows, lanes]
-                    new = factor * total + (1.0 - factor) * tbuf[rows, lanes] + row
-                    acc[rows, lanes] = new
-                    rbuf[q, h, pl.ds(first(me, j), TILE), :] = new.astype(jnp.bfloat16)
+                rows = pl.ds(i * SENT, SENT)
+                parts = [jnp.dot(abuf[slot_of(c), rows, :], rbuf[p, h, pl.ds(first(*order[c]), TILE), :], preferred_element_type=jnp.float32) for c in (30, 31)]
+                new = factor * (acc[rows, lanes] + parts[0]) + factor * parts[1] + (1.0 - factor) * tbuf[rows, lanes] + row
+                acc[rows, lanes] = new
+                rbuf[q, h, pl.ds(first(me, 2 * i), SENT), :] = new.astype(jnp.bfloat16)
 
                 if i == ROWS // SENT - 1:
                     sent = rbuf.at[p, h, pl.ds(0, 28 * TILE), :]

time: 299 us -> 290 us (0.970)
  Pallas kernels: 298 us -> 288 us
    pallas_call x1, Pallas kernels: 298 us -> 288 us  [local_sweeps(): pl.pallas_call(functools.partial(kernel, sweeps), out_shape=pltpu.VMEM((R...]
where the time goes in v8:
time: 290 us
  Pallas kernels  288 us (99%)
    pallas_call x1, Pallas kernels, local_sweeps(): pl.pallas_call(functools.partial(kernel, sweeps), out_shape=pltpu.VMEM((R...  288 us

profile of v8, /device:TPU:0, one launch (start us, length us, event | category | flops | bytes accessed | tf_op | source)
XLA Modules:
  0.0 289.8 jit_solution(11278883276285937622)
XLA Ops:
  0.0 288.5 %sweeps.1 = f32[2048,256]{1,0:T(8,128)S(1)} custom-call(bf16[2048,16384]{1,0:T(8,128)(2,1)} %mat.1, f32[2048,256]{1,0:T(8,128)} %tele.1, s32[16,128]{1,0:T(8,128)} %bitcast.1, f32[8]{0:T(128)} %damp.1, f32[2048,256]{1,0:T(8,128)} %start.1), custom_call_target="tpu_custom_call" | custom-call | tf_op jit(solution)/shard_map/sweeps/pallas_call | solution.py:290
  288.5 1.3 copy.7

commit v9 on v8

--- a/solution.py
+++ b/solution.py
@@ -20,11 +20,11 @@
 MROWS = 1024
 SENT = 1024
 
-X_SLOTS = ((0, 0, 0), (0, 2, 0), (0, 0, 1), (0, 2, 1), (0, 1, 0), (0, 1, 1), (1, 1, 0), (1, 1, 1), (1, 3, 0), (0, 3, 0), (1, 3, 1), (0, 3, 1))
-Y_SLOTS = ((0, 1, 0), (0, 3, 0), (0, 1, 1), (0, 3, 1), (0, 0, 0), (0, 0, 1), (1, 0, 0), (1, 0, 1), (1, 2, 0), (0, 2, 0), (1, 2, 1), (0, 2, 1))
-
-
-def kernel(sweeps, mat, tele, dang, damp, start, acc, factors, rbuf, abuf, tbuf, dcol, draw, mbuf, asem, lsem, ssem, xsem, ysem, dsem, msend, mrecv):
+X_SLOTS = ((0, 0, 0), (0, 2, 0), (0, 0, 1), (0, 2, 1), (0, 1, 2), (1, 1, 2), (1, 3, 0), (0, 3, 0), (1, 3, 1), (0, 3, 1))
+Y_SLOTS = ((0, 1, 0), (0, 3, 0), (0, 1, 1), (0, 3, 1), (0, 0, 2), (1, 0, 2), (1, 2, 0), (0, 2, 0), (1, 2, 1), (0, 2, 1))
+
+
+def kernel(sweeps, mat, tele, dang, damp, start, acc, factors, rbuf, abuf, tbuf, dcol, draw, mpair, mchip, asem, lsem, ssem, xsem, ysem, dsem, msem):
     me = lax.axis_index("row")
     core = lax.rem(me, 2)
     xbit = lax.rem(lax.div(me, 2), 2)
@@ -53,11 +53,11 @@
         return pltpu.make_async_copy(mat.at[:, pl.ds(first(dv, j), TILE)], abuf.at[slot_of(c)], asem.at[slot_of(c)])
 
     def piece(p, dv, j, h):
-        return rbuf.at[p, h, pl.ds(first(dv, j), TILE), :]
+        return rbuf.at[p, slice(None) if h == 2 else h, pl.ds(first(dv, j), TILE), :]
 
     def send(p, dv, j, h, to, recv):
         return pltpu.make_async_remote_copy(
-            src_ref=piece(p, dv, j, h), dst_ref=piece(p, dv, j, h), send_sem=ssem.at[p, h], recv_sem=recv,
+            src_ref=piece(p, dv, j, h), dst_ref=piece(p, dv, j, h), send_sem=ssem.at[p, h % 2], recv_sem=recv,
             device_id={"row": to}, device_id_type=MESH,
         )
 
@@ -83,14 +83,14 @@
         fwd, j, h = Y_SLOTS[k]
         src = dg if fwd else yn
         arrived(p, src, j, h, ysem.at[p, k])
-        send(p, src, j, h, pt, dsem.at[p, 20 + k]).start()
+        send(p, src, j, h, pt, dsem.at[p, 18 + k]).start()
 
     def take_shared(p, ks):
         for k in ks:
             fwd, j, h = X_SLOTS[k]
             arrived(p, pdg if fwd else pxn, j, h, dsem.at[p, 8 + k])
             fwd, j, h = Y_SLOTS[k]
-            arrived(p, pdg if fwd else pyn, j, h, dsem.at[p, 20 + k])
+            arrived(p, pdg if fwd else pyn, j, h, dsem.at[p, 18 + k])
 
     def mass_of(values, rows, h):
         total = None
@@ -101,13 +101,23 @@
             total = part if total is None else total + part
         return jnp.sum(total, axis=0, keepdims=True)
 
+    def mass_copy(ref, sems, to):
+        return pltpu.make_async_remote_copy(
+            src_ref=ref[0], dst_ref=ref[1], send_sem=sems.at[0], recv_sem=sems.at[1], device_id={"row": to}, device_id_type=MESH
+        )
+
     def send_mass(p):
-        for dx, dy, dc in [(a, b, c) for a in range(2) for b in range(2) for c in range(2)][1:]:
-            to = device(lax.rem(xbit + dx, 2), lax.rem(ybit + dy, 2), lax.rem(core + dc, 2))
-            pltpu.make_async_remote_copy(
-                src_ref=mbuf.at[p, me], dst_ref=mbuf.at[p, me], send_sem=msend.at[p], recv_sem=mrecv.at[p],
-                device_id={"row": to}, device_id_type=MESH,
-            ).start()
+        mass_copy((mpair.at[p, 0], mpair.at[p, 1]), msem.at[0, p], pt).start()
+
+    chip = ybit * 2 + xbit
+
+    def chip_mass(p):
+        mass_copy((mpair.at[p, 0], mpair.at[p, 1]), msem.at[0, p], pt).wait()
+        mchip[p, chip] = mpair[p, 0] + mpair[p, 1]
+
+    def send_chip_mass(p):
+        for to in (xn, yn, dg):
+            mass_copy((mchip.at[p, chip], mchip.at[p, chip]), msem.at[1, p], to).start()
 
     def wait_a(t, cs):
         for c in cs:
@@ -182,7 +192,7 @@
             pl.semaphore_wait(barrier, DEV - 1)
             send_x(0, 0)
             send_y(0, 0)
-    for k in range(1, 6):
+    for k in range(1, 5):
         send_x(0, k)
         send_y(0, k)
     for h in range(2):
@@ -197,8 +207,7 @@
             rows = pl.ds(j * TILE, TILE)
             part = mass_of(acc[rows, pl.ds(h * HALF, HALF)], rows, h)
             total = part if total is None else total + part
-        mbuf[0, me, :, pl.ds(h * HALF, HALF)] = total
-    send_mass(0)
+        mpair[0, 0, :, pl.ds(h * HALF, HALF)] = total
     own_tele.wait()
     own_damp.wait()
 
@@ -209,39 +218,42 @@
         for j in range(4):
             for h in range(2):
                 arrived(p, pt, j, h, dsem.at[p, 2 * j + h])
+        send_mass(p)
         matmul(t, p, range(0, 8), init=True)
+        chip_mass(p)
         for k in range(3):
             take(p, k)
-        for k in (6, 7, 8, 9):
+        send_chip_mass(p)
+        for k in (5, 6, 7):
             send_x(p, k)
             send_y(p, k)
         take(p, 3)
-        for k in (10, 11):
+        for k in (8, 9):
             send_x(p, k)
             send_y(p, k)
         matmul(t, p, range(8, 12))
         take_shared(p, range(0, 4))
         matmul(t, p, range(12, 16))
         for s in range(2):
-            take(p, 4 + 2 * s)
-            take(p, 5 + 2 * s)
+            take(p, 4 + s)
             matmul(t, p, range(16 + 4 * s, 18 + 4 * s))
-            take_shared(p, (4 + 2 * s, 5 + 2 * s))
+            take_shared(p, (4 + s,))
             matmul(t, p, range(18 + 4 * s, 20 + 4 * s))
         wait_a(t, range(24, 32))
-        pltpu.make_async_copy(mbuf.at[p, pl.ds(0, DEV - 1)], mbuf.at[p, pl.ds(0, DEV - 1)], mrecv.at[p]).wait()
-        pltpu.make_async_copy(mbuf.at[p, pl.ds(0, DEV - 1)], mbuf.at[p, pl.ds(0, DEV - 1)], msend.at[p]).wait()
-        mass = jnp.sum(mbuf[p], axis=0)
+        others = mchip.at[p, pl.ds(0, 3)]
+        pltpu.make_async_copy(others, others, msem.at[1, p, 1]).wait()
+        pltpu.make_async_copy(others, others, msem.at[1, p, 0]).wait()
+        mass = jnp.sum(mchip[p], axis=0)
         factor = factors[t]
         nodes = DEV * ROWS
         for h in range(2):
-            take(p, 8 + 2 * h)
+            take(p, 6 + 2 * h)
             matmul_half(p, (24, 25), h)
-            take_shared(p, (8 + 2 * h,))
+            take_shared(p, (6 + 2 * h,))
             matmul_half(p, (26, 27), h)
-            take(p, 9 + 2 * h)
+            take(p, 7 + 2 * h)
             matmul_half(p, (28, 29), h)
-            take_shared(p, (9 + 2 * h,))
+            take_shared(p, (7 + 2 * h,))
             lanes = pl.ds(h * HALF, HALF)
             row = (factor / nodes) * mass[:, h * HALF:(h + 1) * HALF]
             for i in range(ROWS // SENT):
@@ -252,7 +264,7 @@
                 rbuf[q, h, pl.ds(first(me, 2 * i), SENT), :] = new.astype(jnp.bfloat16)
 
                 if i == ROWS // SENT - 1:
-                    sent = rbuf.at[p, h, pl.ds(0, 28 * TILE), :]
+                    sent = rbuf.at[p, :, pl.ds(0, 18 * TILE), :] if h == 0 else rbuf.at[p, 1, pl.ds(0, 20 * TILE), :]
                     pltpu.make_async_copy(sent, sent, ssem.at[p, h]).wait()
 
                 @pl.when(t < sweeps - 1)
@@ -262,9 +274,8 @@
                     share_own(q, 2 * i, h)
                     share_own(q, 2 * i + 1, h)
                     if i + h == 2:
-                        for k in (4, 5):
-                            send_x(q, k)
-                            send_y(q, k)
+                        send_x(q, 4)
+                        send_y(q, 4)
 
 
         @pl.when(t < sweeps - 1)
@@ -276,8 +287,7 @@
                     rows = pl.ds(j * TILE, TILE)
                     part = mass_of(acc[rows, lanes], rows, h)
                     held = part if held is None else held + part
-                mbuf[q, me, :, lanes] = held
-            send_mass(q)
+                mpair[q, 0, :, lanes] = held
 
 
 def solution(mesh):
@@ -299,15 +309,15 @@
                 pltpu.VMEM((ROWS, COLS), jnp.float32),
                 pltpu.VMEM((128, 128), jnp.float32),
                 pltpu.VMEM((ROWS // 128, 128), jnp.int32),
-                pltpu.VMEM((2, DEV, 1, COLS), jnp.float32),
+                pltpu.VMEM((2, 2, 1, COLS), jnp.float32),
+                pltpu.VMEM((2, 4, 1, COLS), jnp.float32),
                 pltpu.SemaphoreType.DMA((len(KEPT) + RING,)),
                 pltpu.SemaphoreType.DMA((7,)),
                 pltpu.SemaphoreType.DMA((2, 2)),
-                pltpu.SemaphoreType.DMA((2, 12)),
-                pltpu.SemaphoreType.DMA((2, 12)),
-                pltpu.SemaphoreType.DMA((2, 32)),
-                pltpu.SemaphoreType.DMA((2,)),
-                pltpu.SemaphoreType.DMA((2,)),
+                pltpu.SemaphoreType.DMA((2, 10)),
+                pltpu.SemaphoreType.DMA((2, 10)),
+                pltpu.SemaphoreType.DMA((2, 28)),
+                pltpu.SemaphoreType.DMA((2, 2, 2)),
             ],
             compiler_params=pltpu.CompilerParams(collective_id=0, has_side_effects=True, vmem_limit_bytes=64946176),
             name="sweeps",

time: 290 us -> 289 us (level)
  no operation moved by 1% of the time
where the time goes in v9:
time: 289 us
  Pallas kernels  288 us (100%)
    pallas_call x1, Pallas kernels, local_sweeps(): pl.pallas_call(functools.partial(kernel, sweeps), out_shape=pltpu.VMEM((R...  288 us

profile of v9, /device:TPU:0, one launch (start us, length us, event | category | flops | bytes accessed | tf_op | source)
XLA Modules:
  0.0 289.2 jit_solution(4986102044838428961)
XLA Ops:
  0.0 287.9 %sweeps.1 = f32[2048,256]{1,0:T(8,128)S(1)} custom-call(bf16[2048,16384]{1,0:T(8,128)(2,1)} %mat.1, f32[2048,256]{1,0:T(8,128)} %tele.1, s32[16,128]{1,0:T(8,128)} %bitcast.1, f32[8]{0:T(128)} %damp.1, f32[2048,256]{1,0:T(8,128)} %start.1), custom_call_target="tpu_custom_call" | custom-call | tf_op jit(solution)/shard_map/sweeps/pallas_call | solution.py:300
  287.9 1.3 copy.7
